TPU v7x, 32 devices: a whole 2x2x4 slice. The times are simulated.
32 devices in a mesh: az: 4 (over y, x), rad: 8 (over z, core).
Axes of the slice: x: 2, y: 2, z: 4, core: 2. Of those that a mesh axis runs over, the one named last changes fastest.
Arguments:
- fields: float32 [5, 96, 32, 512], P(None, 'rad', None, 'az'), may hold values from -6 to 6
- shift: int32 [96], replicated, may hold values from 0 to 511
- fraction: float32 [96], replicated, may hold values from -0.5 to 0.5
- radial_rate: float32 [96, 32], replicated, may hold values from -0.4 to 0.4
Outputs:
- updated: float32 [5, 96, 32, 512], P(None, 'rad', None, 'az')
All inputs are finite; a program needn't handle non-finite values.
Results may differ from a plain program's by a relative error of at most 0.0003.
Values sent between devices are 32-bit elements; how exact they have to be, the bound alone decides.
A program may use at most 64 MiB of HBM per device.

v0:
```python
import functools

import jax
import jax.numpy as jnp
from jax import lax
from jax.experimental import pallas as pl
from jax.experimental.pallas import tpu as pltpu
from jax.sharding import PartitionSpec as P

MESH = pl.DeviceIdType.MESH


def half_slope(left, right):
    low = jnp.maximum(jnp.minimum(left, right), 0.0)
    high = jnp.minimum(jnp.maximum(left, right), 0.0)
    return jnp.maximum(jnp.minimum(0.25 * (left + right), low), high)


def chunks_of(fields, rows, group):
    rest = rows // group - 1
    if rest == 0:
        return [(True, f, 1) for f in range(fields)]
    return [(True, 0, fields), (False, 0, fields - 2), (False, fields - 2, 2)]


def peers_of(group, me):
    if group == 4:
        inner = me + 1 - 2 * lax.rem(me, 2)
        outer = lax.rem(me + 2, 4)
        return [inner, outer], [inner + outer - me]
    return [lax.rem(me + step, group) for step in range(1, group)], []


def kernel(
    group, rings, chunks,
    fields, shift_in, fraction_in, rates_in,
    out,
    own, landed, rate, bend, shift, fraction, rates, *rest,
):
    count = len(chunks)
    gathered, results = rest[:count], rest[count : 2 * count]
    small_sem, in_sem, own_sem, send1, recv1, send2, recv2, ghost_send, ghost_recv, passed = rest[2 * count :]
    nf, rows, polar, width = fields.shape
    me, ring = lax.axis_index("az"), lax.axis_index("rad")
    more = rows // group - 1
    start = ring * rows

    def base(first, d):
        if first:
            return jnp.where(d < 2, d, jnp.where(d < 4, rows - 4 + d, d - 2))
        return group - 2 + d * more

    def height(first):
        return 1 if first else more

    near, far = peers_of(group, me)
    barrier = pltpu.get_barrier_semaphore()
    for d in near:
        pl.semaphore_signal(barrier, inc=1, device_id=(d, ring), device_id_type=MESH)

    @pl.when(ring > 0)
    def _():
        pl.semaphore_signal(barrier, inc=1, device_id=(me, ring - 1), device_id_type=MESH)

    @pl.when(ring < rings - 1)
    def _():
        pl.semaphore_signal(barrier, inc=1, device_id=(me, ring + 1), device_id_type=MESH)

    stages = [
        pltpu.make_async_copy(fields.at[:, pl.ds(0, group - 2)], own.at[:, pl.ds(0, group - 2)], in_sem.at[0]),
        pltpu.make_async_copy(fields.at[:, pl.ds(rows - 2, 2)], own.at[:, pl.ds(rows - 2, 2)], in_sem.at[1]),
    ]
    if more:
        stages.append(
            pltpu.make_async_copy(
                fields.at[:, pl.ds(group - 2, rows - group)],
                own.at[:, pl.ds(group - 2, rows - group)],
                in_sem.at[2],
            )
        )
    for copy in stages:
        copy.start()
    mine = []
    for c, (first, f0, n) in enumerate(chunks):
        copy = pltpu.make_async_copy(
            fields.at[pl.ds(f0, n), pl.ds(base(first, me), height(first))],
            gathered[c].at[me],
            own_sem.at[c],
        )
        copy.start()
        mine.append(copy)

    small = [
        pltpu.make_async_copy(rates_in, rates, small_sem.at[0]),
        pltpu.make_async_copy(shift_in, shift, small_sem.at[1]),
        pltpu.make_async_copy(fraction_in, fraction, small_sem.at[2]),
    ]
    for copy in small:
        copy.start()

    neighbours = len(near) + jnp.where(ring > 0, 1, 0) + jnp.where(ring < rings - 1, 1, 0)
    pl.semaphore_wait(barrier, neighbours)
    if far:
        pl.semaphore_signal(passed, inc=1, device_id=(near[0], ring), device_id_type=MESH)

    def out_copy(c, d):
        first, f0, n = chunks[c]
        return pltpu.make_async_remote_copy(
            src_ref=own.at[pl.ds(f0, n), pl.ds(base(first, d), height(first))],
            dst_ref=gathered[c].at[me],
            send_sem=send1.at[c, d],
            recv_sem=recv1.at[c, me],
            device_id=(d, ring),
            device_id_type=MESH,
        )

    def in_copy(c, s):
        first, f0, n = chunks[c]
        return pltpu.make_async_remote_copy(
            src_ref=gathered[c].at[s],
            dst_ref=gathered[c].at[s],
            send_sem=send1.at[c, s],
            recv_sem=recv1.at[c, s],
            device_id=(s, ring),
            device_id_type=MESH,
        )

    def back_copy(c, d):
        first, f0, n = chunks[c]
        return pltpu.make_async_remote_copy(
            src_ref=results[c].at[d],
            dst_ref=landed.at[pl.ds(f0, n), pl.ds(2 + base(first, me), height(first))],
            send_sem=send2.at[c, d],
            recv_sem=recv2.at[c, me],
            device_id=(d, ring),
            device_id_type=MESH,
        )

    def home_copy(c, s):
        first, f0, n = chunks[c]
        target = landed.at[pl.ds(f0, n), pl.ds(2 + base(first, s), height(first))]
        return pltpu.make_async_remote_copy(
            src_ref=target,
            dst_ref=target,
            send_sem=send2.at[c, s],
            recv_sem=recv2.at[c, s],
            device_id=(s, ring),
            device_id_type=MESH,
        )

    def peers():
        return far + near

    def ready(c):
        if c == 0:
            stages[0].wait()
            stages[1].wait()
        if c == 1 and more:
            stages[2].wait()

    for c in range(min(2, count)):
        ready(c)
        for d in near:
            out_copy(c, d).start()
    if far:
        pl.semaphore_wait(passed, 1)
    for c in range(count):
        for d in far:
            out_copy(c, d).start()
        if c > 1:
            for d in near:
                out_copy(c, d).start()

    small[0].wait()
    table = rates[...]
    place = lax.broadcasted_iota(jnp.int32, table.shape, 1)
    for j in range(rows + 1):
        column = jnp.sum(
            jnp.where(place == start - 1 + j, table, 0.0), axis=1, keepdims=True
        )
        if j == 0:
            column = jnp.where(ring > 0, column, 0.0)
        if j == rows:
            column = jnp.where(ring < rings - 1, column, 0.0)
        spread = jnp.broadcast_to(column, (polar, width))
        size = jnp.abs(spread)
        rate[j] = spread
        bend[j] = size * (1.0 - size)

    @pl.when(ring == 0)
    def _():
        landed[:, 0:2] = jnp.zeros((nf, 2, polar, width), jnp.float32)

    @pl.when(ring == rings - 1)
    def _():
        landed[:, rows + 2 : rows + 4] = jnp.zeros((nf, 2, polar, width), jnp.float32)

    lane = lax.broadcasted_iota(jnp.int32, (polar, width), 1)
    at_first, at_last = lane == 0, lane == width - 1

    def previous(blocks):
        turned = [pltpu.roll(b, 1, 1) for b in blocks]
        return [jnp.where(at_first, turned[p - 1], turned[p]) for p in range(group)]

    def following(blocks):
        turned = [pltpu.roll(b, width - 1, 1) for b in blocks]
        return [jnp.where(at_last, turned[(p + 1) % group], turned[p]) for p in range(group)]

    cycle = group * width

    def azimuth(c):
        first, f0, n = chunks[c]
        source, target = gathered[c], results[c]
        for k in range(height(first)):
            row = start + base(first, me) + k
            courant = fraction[row]
            ahead = courant > 0.0
            amount = shift[row] + jnp.where(ahead, cycle, cycle - 1)
            whole = lax.rem(amount // width, group)
            part = lax.rem(amount, width)
            size = jnp.abs(courant)
            bent = size * (1.0 - size)
            beyond = lane >= part

            for f in range(n):
                turned = [
                    pltpu.roll(source[lax.rem(p + group - whole, group), f, k], part, 1)
                    for p in range(group)
                ]
                q = [jnp.where(beyond, turned[p], turned[p - 1]) for p in range(group)]
                before = previous(q)
                left = [x - y for x, y in zip(q, before)]
                right = following(left)
                value = [
                    courant * x + bent * half_slope(l, r) for x, l, r in zip(q, left, right)
                ]
                lower = previous(value)
                for p in range(group):
                    kept = jnp.where(ahead, q[p], before[p])
                    target[p, f, k] = kept - (value[p] - lower[p])
        landed[pl.ds(f0, n), pl.ds(2 + base(first, me), height(first))] = target[me]

    ghosts = [
        pltpu.make_async_remote_copy(
            src_ref=landed.at[:, pl.ds(2, 2)],
            dst_ref=landed.at[:, pl.ds(rows + 2, 2)],
            send_sem=ghost_send.at[0],
            recv_sem=ghost_recv.at[0],
            device_id=(me, jnp.maximum(ring - 1, 0)),
            device_id_type=MESH,
        ),
        pltpu.make_async_remote_copy(
            src_ref=landed.at[:, pl.ds(rows, 2)],
            dst_ref=landed.at[:, pl.ds(0, 2)],
            send_sem=ghost_send.at[1],
            recv_sem=ghost_recv.at[1],
            device_id=(me, jnp.minimum(ring + 1, rings - 1)),
            device_id_type=MESH,
        ),
    ]

    def radial(f):
        def cell(i):
            return landed[f, i]

        q1, q2 = cell(1), cell(2)
        d1 = q1 - cell(0)
        d2 = q2 - q1
        h1 = half_slope(d1, d2)
        below = None
        for j in range(rows + 1):
            q3 = cell(j + 3)
            d3 = q3 - q2
            h2 = half_slope(d2, d3)
            c, b = rate[j], bend[j]
            ahead = c > 0.0
            flux = c * jnp.where(ahead, q1, q2) + b * jnp.where(ahead, h1, h2)
            if j > 0:
                out[f, j - 1] = q1 - (flux - below)
            below = flux
            q1, q2, d2, h1 = q2, q3, d3, h2

    edges = 1 if more else count

    small[1].wait()
    small[2].wait()
    for c in range(count):
        mine[c].wait()
        for s in peers():
            in_copy(c, s).wait_recv()
        azimuth(c)
        for d in peers():
            back_copy(c, d).start()

    for c in range(edges):
        for s in peers():
            home_copy(c, s).wait_recv()

    @pl.when(ring > 0)
    def _():
        ghosts[0].start()

    @pl.when(ring < rings - 1)
    def _():
        ghosts[1].start()

    @pl.when(ring > 0)
    def _():
        ghosts[1].wait_recv()

    @pl.when(ring < rings - 1)
    def _():
        ghosts[0].wait_recv()

    for c in range(edges, count):
        first, f0, n = chunks[c]
        for s in peers():
            home_copy(c, s).wait_recv()
        for f in range(f0, f0 + n):
            radial(f)
    if not more:
        for f in range(nf):
            radial(f)

    for c in range(count):
        for d in peers():
            out_copy(c, d).wait_send()
            back_copy(c, d).wait_send()

    @pl.when(ring > 0)
    def _():
        ghosts[0].wait_send()

    @pl.when(ring < rings - 1)
    def _():
        ghosts[1].wait_send()


def shards(fields, shift, fraction, radial_rate):
    nf, rows, polar, width = fields.shape
    group, rings = lax.axis_size("az"), lax.axis_size("rad")
    chunks = chunks_of(nf, rows, group)
    more = rows // group - 1
    boxes = [
        pltpu.VMEM((group, n, 1 if first else more, polar, width), jnp.float32)
        for first, f0, n in chunks
    ]
    count = len(chunks)
    dma = pltpu.SemaphoreType.DMA
    operands = (fields, shift, fraction, radial_rate.T)
    return pl.pallas_call(
        functools.partial(kernel, group, rings, chunks),
        out_shape=jax.ShapeDtypeStruct(fields.shape, jnp.float32),
        in_specs=[pl.BlockSpec(memory_space=pltpu.HBM)] * 4,
        out_specs=pl.BlockSpec(memory_space=pltpu.VMEM),
        scratch_shapes=[
            pltpu.VMEM((nf, rows, polar, width), jnp.float32),
            pltpu.VMEM((nf, rows + 4, polar, width), jnp.float32),
            pltpu.VMEM((rows + 1, polar, width), jnp.float32),
            pltpu.VMEM((rows + 1, polar, width), jnp.float32),
            pltpu.SMEM(shift.shape, jnp.int32),
            pltpu.SMEM(fraction.shape, jnp.float32),
            pltpu.VMEM(radial_rate.shape[::-1], jnp.float32),
            *boxes,
            *boxes,
            dma((3,)),
            dma((3,)),
            dma((count,)),
            dma((count, group)),
            dma((count, group)),
            dma((count, group)),
            dma((count, group)),
            dma((2,)),
            dma((2,)),
            pltpu.SemaphoreType.REGULAR,
        ],
        compiler_params=pltpu.CompilerParams(
            collective_id=0, has_side_effects=True, vmem_limit_bytes=10 * fields.size * 4
        ),
    )(*(pltpu.with_memory_space_constraint(x, pltpu.HBM) for x in operands))


def solution(mesh):
    placed = (P(None, "rad", None, "az"), P(), P(), P())
    return jax.shard_map(
        shards, mesh=mesh, in_specs=placed, out_specs=P(None, "rad", None, "az"), check_vma=False
    )
```

profile of v0, /device:TPU:0, one launch (start us, length us, event | category | flops | bytes accessed | tf_op | source)
XLA Modules:
  0.0 28.5 jit_solution(14280949964165225302)
XLA Ops:
  0.0 27.5 %shard_map.46 = f32[5,12,32,128]{3,2,1,0:T(8,128)S(1)} custom-call(f32[5,12,32,128]{3,2,1,0:T(8,128)} %fields.1, s32[96]{0:T(128)} %shift_in.1, f32[96]{0:T(128)} %fraction_in.1, f32[32,96]{1,0:T(8,128)} %bitcast.1), custom_call_target="tpu_custom_call" | custom-call | tf_op jit(solution)/shard_map/pallas_call | solution.py:351
  27.5 0.9 %copy.6 = f32[5,12,32,128]{3,2,1,0:T(8,128)} copy(f32[5,12,32,128]{3,2,1,0:T(8,128)S(1)} %shard_map.46) | data formatting | bytes 1966080
where the time goes:
time: 28.6 us; the launch traced here: 28.5 us
  Pallas kernels  27.5 us (96%)
  local copies, waits for them, and re-layouts  0.95 us (3%)
    pallas_call x1, Pallas kernels, shards(): pl.pallas_call(functools.partial(kernel, group, rings, chunks), out_shape...  27.5 us
    unnamed x1, local copies, waits for them, and re-layouts  0.95 us

commit v1 on v0

--- a/solution.py
+++ b/solution.py
@@ -39,7 +39,7 @@
 ):
     count = len(chunks)
     gathered, results = rest[:count], rest[count : 2 * count]
-    small_sem, in_sem, own_sem, send1, recv1, send2, recv2, ghost_send, ghost_recv, passed = rest[2 * count :]
+    small_sem, in_sem, own_sem, send1, recv1, send2, recv2, ghost_send, ghost_recv, passed, from_above, from_below, clear = rest[2 * count :]
     nf, rows, polar, width = fields.shape
     me, ring = lax.axis_index("az"), lax.axis_index("rad")
     more = rows // group - 1
@@ -58,13 +58,16 @@
     for d in near:
         pl.semaphore_signal(barrier, inc=1, device_id=(d, ring), device_id_type=MESH)
 
-    @pl.when(ring > 0)
-    def _():
-        pl.semaphore_signal(barrier, inc=1, device_id=(me, ring - 1), device_id_type=MESH)
-
-    @pl.when(ring < rings - 1)
-    def _():
-        pl.semaphore_signal(barrier, inc=1, device_id=(me, ring + 1), device_id_type=MESH)
+    below, above = ring > 0, ring < rings - 1
+    leads = me == 0
+
+    def tell(who, semaphore, step):
+        @pl.when(who)
+        def _():
+            pl.semaphore_signal(semaphore, inc=1, device_id=(me, ring + step), device_id_type=MESH)
+
+    lowers, lifts = jnp.logical_and(leads, below), jnp.logical_and(leads, above)
+    tell(lifts, barrier, 1)
 
     stages = [
         pltpu.make_async_copy(fields.at[:, pl.ds(0, group - 2)], own.at[:, pl.ds(0, group - 2)], in_sem.at[0]),
@@ -98,8 +101,8 @@
     for copy in small:
         copy.start()
 
-    neighbours = len(near) + jnp.where(ring > 0, 1, 0) + jnp.where(ring < rings - 1, 1, 0)
-    pl.semaphore_wait(barrier, neighbours)
+    with jax.named_scope("barrier"):
+        pl.semaphore_wait(barrier, len(near) + jnp.where(lowers, 1, 0))
     if far:
         pl.semaphore_signal(passed, inc=1, device_id=(near[0], ring), device_id_type=MESH)
 
@@ -163,7 +166,9 @@
         for d in near:
             out_copy(c, d).start()
     if far:
-        pl.semaphore_wait(passed, 1)
+        with jax.named_scope("passed"):
+            pl.semaphore_wait(passed, 1)
+    tell(lowers, from_above, -1)
     for c in range(count):
         for d in far:
             out_copy(c, d).start()
@@ -284,17 +289,40 @@
 
     small[1].wait()
     small[2].wait()
+
+    @pl.when(lifts)
+    def _():
+        pl.semaphore_wait(from_above, 1)
+
+    tell(lifts, from_below, 1)
     for c in range(count):
-        mine[c].wait()
-        for s in peers():
-            in_copy(c, s).wait_recv()
-        azimuth(c)
+        with jax.named_scope("arrived"):
+            mine[c].wait()
+            for s in peers():
+                in_copy(c, s).wait_recv()
+        with jax.named_scope("azimuth"):
+            azimuth(c)
         for d in peers():
             back_copy(c, d).start()
-
-    for c in range(edges):
-        for s in peers():
-            home_copy(c, s).wait_recv()
+        if c == 0:
+
+            @pl.when(lowers)
+            def _():
+                pl.semaphore_wait(from_below, 1)
+
+            @pl.when(leads)
+            def _():
+                for d in peers():
+                    pl.semaphore_signal(clear, inc=1, device_id=(d, ring), device_id_type=MESH)
+
+    @pl.when(jnp.logical_not(leads))
+    def _():
+        pl.semaphore_wait(clear, 1)
+
+    with jax.named_scope("home"):
+        for c in range(edges):
+            for s in peers():
+                home_copy(c, s).wait_recv()
 
     @pl.when(ring > 0)
     def _():
@@ -314,10 +342,12 @@
 
     for c in range(edges, count):
         first, f0, n = chunks[c]
-        for s in peers():
-            home_copy(c, s).wait_recv()
-        for f in range(f0, f0 + n):
-            radial(f)
+        with jax.named_scope("home"):
+            for s in peers():
+                home_copy(c, s).wait_recv()
+        with jax.named_scope("radial"):
+            for f in range(f0, f0 + n):
+                radial(f)
     if not more:
         for f in range(nf):
             radial(f)
@@ -372,7 +402,7 @@
             dma((count, group)),
             dma((2,)),
             dma((2,)),
-            pltpu.SemaphoreType.REGULAR,
+            *[pltpu.SemaphoreType.REGULAR] * 4,
         ],
         compiler_params=pltpu.CompilerParams(
             collective_id=0, has_side_effects=True, vmem_limit_bytes=10 * fields.size * 4

time: 28.6 us -> 28 us (0.979)
  Pallas kernels: 27.5 us -> 26.9 us
    pallas_call x1, Pallas kernels: 27.5 us -> 26.9 us  [shards(): pl.pallas_call(functools.partial(kernel, group, rings, chunks), out_shape...]
where the time goes in v1:
time: 28 us; the launch traced here: 27.9 us
  Pallas kernels  26.9 us (96%)
  local copies, waits for them, and re-layouts  0.95 us (3%)
    pallas_call x1, Pallas kernels, shards(): pl.pallas_call(functools.partial(kernel, group, rings, chunks), out_shape...  26.9 us
    unnamed x1, local copies, waits for them, and re-layouts  0.95 us

profile of v1, /device:TPU:0, one launch (start us, length us, event | category | flops | bytes accessed | tf_op | source)
XLA Modules:
  0.0 27.9 jit_solution(16378036677984432680)
XLA Ops:
  0.0 26.9 %shard_map.46 = f32[5,12,32,128]{3,2,1,0:T(8,128)S(1)} custom-call(f32[5,12,32,128]{3,2,1,0:T(8,128)} %fields.1, s32[96]{0:T(128)} %shift_in.1, f32[96]{0:T(128)} %fraction_in.1, f32[32,96]{1,0:T(8,128)} %bitcast.1), custom_call_target="tpu_custom_call" | custom-call | tf_op jit(solution)/shard_map/pallas_call | solution.py:381
  26.9 0.9 %copy.6 = f32[5,12,32,128]{3,2,1,0:T(8,128)} copy(f32[5,12,32,128]{3,2,1,0:T(8,128)S(1)} %shard_map.46) | data formatting | bytes 1966080

commit v2 on v1

--- a/solution.py
+++ b/solution.py
@@ -39,7 +39,7 @@
 ):
     count = len(chunks)
     gathered, results = rest[:count], rest[count : 2 * count]
-    small_sem, in_sem, own_sem, send1, recv1, send2, recv2, ghost_send, ghost_recv, passed, from_above, from_below, clear = rest[2 * count :]
+    small_sem, in_sem, sent, gather_sem, home_sem, ghost_send, ghost_recv, passed, told, from_below = rest[2 * count :]
     nf, rows, polar, width = fields.shape
     me, ring = lax.axis_index("az"), lax.axis_index("rad")
     more = rows // group - 1
@@ -71,27 +71,24 @@
 
     stages = [
         pltpu.make_async_copy(fields.at[:, pl.ds(0, group - 2)], own.at[:, pl.ds(0, group - 2)], in_sem.at[0]),
-        pltpu.make_async_copy(fields.at[:, pl.ds(rows - 2, 2)], own.at[:, pl.ds(rows - 2, 2)], in_sem.at[1]),
+        pltpu.make_async_copy(fields.at[:, pl.ds(rows - 2, 2)], own.at[:, pl.ds(rows - 2, 2)], in_sem.at[0]),
     ]
     if more:
         stages.append(
             pltpu.make_async_copy(
                 fields.at[:, pl.ds(group - 2, rows - group)],
                 own.at[:, pl.ds(group - 2, rows - group)],
-                in_sem.at[2],
+                in_sem.at[1],
             )
         )
     for copy in stages:
         copy.start()
-    mine = []
     for c, (first, f0, n) in enumerate(chunks):
-        copy = pltpu.make_async_copy(
+        pltpu.make_async_copy(
             fields.at[pl.ds(f0, n), pl.ds(base(first, me), height(first))],
             gathered[c].at[me],
-            own_sem.at[c],
-        )
-        copy.start()
-        mine.append(copy)
+            gather_sem.at[c],
+        ).start()
 
     small = [
         pltpu.make_async_copy(rates_in, rates, small_sem.at[0]),
@@ -106,58 +103,44 @@
     if far:
         pl.semaphore_signal(passed, inc=1, device_id=(near[0], ring), device_id_type=MESH)
 
+    def remote(src, dst, send_sem, recv_sem, device):
+        return pltpu.make_async_remote_copy(
+            src_ref=src, dst_ref=dst, send_sem=send_sem, recv_sem=recv_sem,
+            device_id=device, device_id_type=MESH,
+        )
+
     def out_copy(c, d):
         first, f0, n = chunks[c]
-        return pltpu.make_async_remote_copy(
-            src_ref=own.at[pl.ds(f0, n), pl.ds(base(first, d), height(first))],
-            dst_ref=gathered[c].at[me],
-            send_sem=send1.at[c, d],
-            recv_sem=recv1.at[c, me],
-            device_id=(d, ring),
-            device_id_type=MESH,
-        )
-
-    def in_copy(c, s):
-        first, f0, n = chunks[c]
-        return pltpu.make_async_remote_copy(
-            src_ref=gathered[c].at[s],
-            dst_ref=gathered[c].at[s],
-            send_sem=send1.at[c, s],
-            recv_sem=recv1.at[c, s],
-            device_id=(s, ring),
-            device_id_type=MESH,
+        return remote(
+            own.at[pl.ds(f0, n), pl.ds(base(first, d), height(first))],
+            gathered[c].at[me], sent.at[0], gather_sem.at[c], (d, ring),
         )
 
     def back_copy(c, d):
         first, f0, n = chunks[c]
-        return pltpu.make_async_remote_copy(
-            src_ref=results[c].at[d],
-            dst_ref=landed.at[pl.ds(f0, n), pl.ds(2 + base(first, me), height(first))],
-            send_sem=send2.at[c, d],
-            recv_sem=recv2.at[c, me],
-            device_id=(d, ring),
-            device_id_type=MESH,
-        )
-
-    def home_copy(c, s):
-        first, f0, n = chunks[c]
-        target = landed.at[pl.ds(f0, n), pl.ds(2 + base(first, s), height(first))]
-        return pltpu.make_async_remote_copy(
-            src_ref=target,
-            dst_ref=target,
-            send_sem=send2.at[c, s],
-            recv_sem=recv2.at[c, s],
-            device_id=(s, ring),
-            device_id_type=MESH,
-        )
+        return remote(
+            results[c].at[d],
+            landed.at[pl.ds(f0, n), pl.ds(2 + base(first, me), height(first))],
+            sent.at[1], home_sem.at[c], (d, ring),
+        )
+
+    def bytes_of(ref, semaphore):
+        return remote(ref, ref, semaphore, semaphore, (me, ring))
+
+    def arrive(c):
+        with jax.named_scope("arrived"):
+            bytes_of(gathered[c], gather_sem.at[c]).wait_recv()
+
+    def home(c):
+        with jax.named_scope("home"):
+            bytes_of(results[c].at[pl.ds(0, group - 1)], home_sem.at[c]).wait_recv()
 
     def peers():
         return far + near
 
     def ready(c):
         if c == 0:
-            stages[0].wait()
-            stages[1].wait()
+            bytes_of(own.at[:, pl.ds(0, group)], in_sem.at[0]).wait_recv()
         if c == 1 and more:
             stages[2].wait()
 
@@ -168,7 +151,7 @@
     if far:
         with jax.named_scope("passed"):
             pl.semaphore_wait(passed, 1)
-    tell(lowers, from_above, -1)
+    tell(lowers, told, -1)
     for c in range(count):
         for d in far:
             out_copy(c, d).start()
@@ -246,22 +229,13 @@
         landed[pl.ds(f0, n), pl.ds(2 + base(first, me), height(first))] = target[me]
 
     ghosts = [
-        pltpu.make_async_remote_copy(
-            src_ref=landed.at[:, pl.ds(2, 2)],
-            dst_ref=landed.at[:, pl.ds(rows + 2, 2)],
-            send_sem=ghost_send.at[0],
-            recv_sem=ghost_recv.at[0],
-            device_id=(me, jnp.maximum(ring - 1, 0)),
-            device_id_type=MESH,
-        ),
-        pltpu.make_async_remote_copy(
-            src_ref=landed.at[:, pl.ds(rows, 2)],
-            dst_ref=landed.at[:, pl.ds(0, 2)],
-            send_sem=ghost_send.at[1],
-            recv_sem=ghost_recv.at[1],
-            device_id=(me, jnp.minimum(ring + 1, rings - 1)),
-            device_id_type=MESH,
-        ),
+        remote(landed.at[:, pl.ds(2, 2)], landed.at[:, pl.ds(rows + 2, 2)], ghost_send, ghost_recv, (me, jnp.maximum(ring - 1, 0))),
+        remote(landed.at[:, pl.ds(rows, 2)], landed.at[:, pl.ds(0, 2)], ghost_send, ghost_recv, (me, jnp.minimum(ring + 1, rings - 1))),
+    ]
+    inside = jnp.logical_and(below, above)
+    ghost_bytes = [
+        (inside, bytes_of(landed.at[:, pl.ds(0, 4)], ghost_recv), bytes_of(landed.at[:, pl.ds(0, 4)], ghost_send)),
+        (below != above, bytes_of(landed.at[:, pl.ds(0, 2)], ghost_recv), bytes_of(landed.at[:, pl.ds(0, 2)], ghost_send)),
     ]
 
     def radial(f):
@@ -292,14 +266,11 @@
 
     @pl.when(lifts)
     def _():
-        pl.semaphore_wait(from_above, 1)
+        pl.semaphore_wait(told, 1)
 
     tell(lifts, from_below, 1)
     for c in range(count):
-        with jax.named_scope("arrived"):
-            mine[c].wait()
-            for s in peers():
-                in_copy(c, s).wait_recv()
+        arrive(c)
         with jax.named_scope("azimuth"):
             azimuth(c)
         for d in peers():
@@ -313,38 +284,29 @@
             @pl.when(leads)
             def _():
                 for d in peers():
-                    pl.semaphore_signal(clear, inc=1, device_id=(d, ring), device_id_type=MESH)
+                    pl.semaphore_signal(told, inc=1, device_id=(d, ring), device_id_type=MESH)
 
     @pl.when(jnp.logical_not(leads))
     def _():
-        pl.semaphore_wait(clear, 1)
-
-    with jax.named_scope("home"):
-        for c in range(edges):
-            for s in peers():
-                home_copy(c, s).wait_recv()
-
-    @pl.when(ring > 0)
+        pl.semaphore_wait(told, 1)
+
+    for c in range(edges):
+        home(c)
+
+    @pl.when(below)
     def _():
         ghosts[0].start()
 
-    @pl.when(ring < rings - 1)
+    @pl.when(above)
     def _():
         ghosts[1].start()
 
-    @pl.when(ring > 0)
-    def _():
-        ghosts[1].wait_recv()
-
-    @pl.when(ring < rings - 1)
-    def _():
-        ghosts[0].wait_recv()
+    for case, received, _ in ghost_bytes:
+        pl.when(case)(received.wait_recv)
 
     for c in range(edges, count):
         first, f0, n = chunks[c]
-        with jax.named_scope("home"):
-            for s in peers():
-                home_copy(c, s).wait_recv()
+        home(c)
         with jax.named_scope("radial"):
             for f in range(f0, f0 + n):
                 radial(f)
@@ -352,18 +314,10 @@
         for f in range(nf):
             radial(f)
 
-    for c in range(count):
-        for d in peers():
-            out_copy(c, d).wait_send()
-            back_copy(c, d).wait_send()
-
-    @pl.when(ring > 0)
-    def _():
-        ghosts[0].wait_send()
-
-    @pl.when(ring < rings - 1)
-    def _():
-        ghosts[1].wait_send()
+    for phase in range(2):
+        bytes_of(own.at[:, pl.ds(0, rows - rows // group)], sent.at[phase]).wait_send()
+    for case, _, delivered in ghost_bytes:
+        pl.when(case)(delivered.wait_send)
 
 
 def shards(fields, shift, fraction, radial_rate):
@@ -394,15 +348,13 @@
             *boxes,
             *boxes,
             dma((3,)),
-            dma((3,)),
-            dma((count,)),
-            dma((count, group)),
-            dma((count, group)),
-            dma((count, group)),
-            dma((count, group)),
             dma((2,)),
             dma((2,)),
-            *[pltpu.SemaphoreType.REGULAR] * 4,
+            dma((count,)),
+            dma((count,)),
+            dma,
+            dma,
+            *[pltpu.SemaphoreType.REGULAR] * 3,
         ],
         compiler_params=pltpu.CompilerParams(
             collective_id=0, has_side_effects=True, vmem_limit_bytes=10 * fields.size * 4

time: 28 us -> 27.6 us (0.986)
  Pallas kernels: 26.9 us -> 26.5 us
    pallas_call x1, Pallas kernels: 26.9 us -> 26.5 us  [shards(): pl.pallas_call(functools.partial(kernel, group, rings, chunks), out_shape...]
where the time goes in v2:
time: 27.6 us; the launch traced here: 27.4 us
  Pallas kernels  26.5 us (96%)
  local copies, waits for them, and re-layouts  0.95 us (3%)
    pallas_call x1, Pallas kernels, shards(): pl.pallas_call(functools.partial(kernel, group, rings, chunks), out_shape...  26.5 us
    unnamed x1, local copies, waits for them, and re-layouts  0.95 us

profile of v2, /device:TPU:0, one launch (start us, length us, event | category | flops | bytes accessed | tf_op | source)
XLA Modules:
  0.0 27.4 jit_solution(8930122220958340223)
XLA Ops:
  0.0 26.5 %shard_map.46 = f32[5,12,32,128]{3,2,1,0:T(8,128)S(1)} custom-call(f32[5,12,32,128]{3,2,1,0:T(8,128)} %fields.1, s32[96]{0:T(128)} %shift_in.1, f32[96]{0:T(128)} %fraction_in.1, f32[32,96]{1,0:T(8,128)} %bitcast.1), custom_call_target="tpu_custom_call" | custom-call | tf_op jit(solution)/shard_map/pallas_call | solution.py:335
  26.5 0.9 %copy.6 = f32[5,12,32,128]{3,2,1,0:T(8,128)} copy(f32[5,12,32,128]{3,2,1,0:T(8,128)S(1)} %shard_map.46) | data formatting | bytes 1966080

commit v3 on v2

--- a/solution.py
+++ b/solution.py
@@ -20,7 +20,45 @@
     rest = rows // group - 1
     if rest == 0:
         return [(True, f, 1) for f in range(fields)]
+    if lends(rows, group):
+        return [(True, 0, fields), (False, 0, fields - 2), (False, fields - 2, 1), (False, fields - 1, 1)]
     return [(True, 0, fields), (False, 0, fields - 2), (False, fields - 2, 2)]
+
+
+def lends(rows, group):
+    return group == 4 and rows > group
+
+
+def radial(landed, rate, bend, f, target, g):
+    rows = rate.shape[0] - 1
+    q1, q2 = landed[f, 1], landed[f, 2]
+    d1 = q1 - landed[f, 0]
+    d2 = q2 - q1
+    h1 = half_slope(d1, d2)
+    inner = None
+    for j in range(rows + 1):
+        q3 = landed[f, j + 3]
+        d3 = q3 - q2
+        h2 = half_slope(d2, d3)
+        c, b = rate[j], bend[j]
+        ahead = c > 0.0
+        flux = c * jnp.where(ahead, q1, q2) + b * jnp.where(ahead, h1, h2)
+        if j > 0:
+            target[g, j - 1] = q1 - (flux - inner)
+        inner = flux
+        q1, q2, d2, h1 = q2, q3, d3, h2
+
+
+def finish(done, landed, rate, bend, out, fresh, sems):
+    ready = done.shape[0]
+    early = pltpu.make_async_copy(done, out.at[pl.ds(0, ready)], sems.at[0])
+    late = pltpu.make_async_copy(fresh, out.at[pl.ds(ready, fresh.shape[0])], sems.at[1])
+    early.start()
+    for g in range(fresh.shape[0]):
+        radial(landed, rate, bend, ready + g, fresh, g)
+    late.start()
+    early.wait()
+    late.wait()
 
 
 def peers_of(group, me):
@@ -34,12 +72,16 @@
 def kernel(
     group, rings, chunks,
     fields, shift_in, fraction_in, rates_in,
-    out,
-    own, landed, rate, bend, shift, fraction, rates, *rest,
+    out, landed, rate, bend,
+    own, shift, fraction, rates, *rest,
 ):
     count = len(chunks)
     gathered, results = rest[:count], rest[count : 2 * count]
-    small_sem, in_sem, sent, gather_sem, home_sem, ghost_send, ghost_recv, passed, told, from_below = rest[2 * count :]
+    small_sem, in_sem, sent, gather_sem, home_sem, ghost_send, ghost_recv, passed, told, from_below, *lent = rest[2 * count :]
+    lending = lends(fields.shape[1], group)
+    if lending:
+        lent, lent_sem = lent
+        lent_in, lent_out = lent.at[pl.ds(0, group)], lent.at[pl.ds(group, group)]
     nf, rows, polar, width = fields.shape
     me, ring = lax.axis_index("az"), lax.axis_index("rad")
     more = rows // group - 1
@@ -52,6 +94,10 @@
 
     def height(first):
         return 1 if first else more
+
+    def block(c, d, lift=0):
+        first, f0, n = chunks[c]
+        return pl.ds(f0, n), pl.ds(lift + base(first, d), height(first))
 
     near, far = peers_of(group, me)
     barrier = pltpu.get_barrier_semaphore()
@@ -83,12 +129,23 @@
         )
     for copy in stages:
         copy.start()
-    for c, (first, f0, n) in enumerate(chunks):
-        pltpu.make_async_copy(
-            fields.at[pl.ds(f0, n), pl.ds(base(first, me), height(first))],
-            gathered[c].at[me],
-            gather_sem.at[c],
-        ).start()
+    lender = ring == 0
+    keeps = jnp.logical_or(me != 0, jnp.logical_not(lender))
+    helps = jnp.logical_and(me == 3, lender)
+    usual = jnp.logical_and(keeps, jnp.logical_not(helps))
+
+    def own_copy(c):
+        return pltpu.make_async_copy(fields.at[block(c, me)], gathered[c].at[me], gather_sem.at[c])
+
+    full = count - 1 if lending else count
+    for c in range(full):
+        own_copy(c).start()
+    if lending:
+        pl.when(keeps)(own_copy(full).start)
+
+        @pl.when(helps)
+        def _():
+            pltpu.make_async_copy(fields.at[block(full, 0)], lent_in.at[me], lent_sem).start()
 
     small = [
         pltpu.make_async_copy(rates_in, rates, small_sem.at[0]),
@@ -110,19 +167,20 @@
         )
 
     def out_copy(c, d):
-        first, f0, n = chunks[c]
         return remote(
-            own.at[pl.ds(f0, n), pl.ds(base(first, d), height(first))],
-            gathered[c].at[me], sent.at[0], gather_sem.at[c], (d, ring),
+            own.at[block(c, d)], gathered[c].at[me], sent.at[0, c], gather_sem.at[c], (d, ring)
         )
 
     def back_copy(c, d):
-        first, f0, n = chunks[c]
         return remote(
-            results[c].at[d],
-            landed.at[pl.ds(f0, n), pl.ds(2 + base(first, me), height(first))],
-            sent.at[1], home_sem.at[c], (d, ring),
+            results[c].at[d], landed.at[block(c, me, 2)], sent.at[1 if c < full else 0, c], home_sem.at[c], (d, ring)
         )
+
+    def lend():
+        return remote(own.at[block(full, 0)], lent_in.at[me], sent.at[0, full], lent_sem, (3, ring))
+
+    def give_back(d):
+        return remote(lent_out.at[d], landed.at[block(full, 0, 2)], sent.at[0, full], home_sem.at[full], (d, ring))
 
     def bytes_of(ref, semaphore):
         return remote(ref, ref, semaphore, semaphore, (me, ring))
@@ -133,7 +191,11 @@
 
     def home(c):
         with jax.named_scope("home"):
-            bytes_of(results[c].at[pl.ds(0, group - 1)], home_sem.at[c]).wait_recv()
+            if c < full:
+                bytes_of(results[c].at[pl.ds(0, group - 1)], home_sem.at[c]).wait_recv()
+                return
+            for who, pieces in ((jnp.logical_not(keeps), 4), (helps, 2), (usual, 3)):
+                pl.when(who)(bytes_of(results[c].at[pl.ds(0, pieces)], home_sem.at[c]).wait_recv)
 
     def peers():
         return far + near
@@ -144,7 +206,8 @@
         if c == 1 and more:
             stages[2].wait()
 
-    for c in range(min(2, count)):
+    started = min(2, count)
+    for c in range(started):
         ready(c)
         for d in near:
             out_copy(c, d).start()
@@ -152,12 +215,17 @@
         with jax.named_scope("passed"):
             pl.semaphore_wait(passed, 1)
     tell(lowers, told, -1)
-    for c in range(count):
+    for c in range(started):
         for d in far:
             out_copy(c, d).start()
-        if c > 1:
-            for d in near:
-                out_copy(c, d).start()
+    if lending:
+        pl.when(jnp.logical_and(lender, me != 3))(lend().start)
+    for c in range(started, full):
+        for d in near + far:
+            out_copy(c, d).start()
+    if lending:
+        for d in near + far:
+            pl.when(jnp.logical_or(d != 0, jnp.logical_not(lender)))(out_copy(full, d).start)
 
     small[0].wait()
     table = rates[...]
@@ -196,11 +264,10 @@
 
     cycle = group * width
 
-    def azimuth(c):
+    def azimuth(c, source, target, owner):
         first, f0, n = chunks[c]
-        source, target = gathered[c], results[c]
         for k in range(height(first)):
-            row = start + base(first, me) + k
+            row = start + base(first, owner) + k
             courant = fraction[row]
             ahead = courant > 0.0
             amount = shift[row] + jnp.where(ahead, cycle, cycle - 1)
@@ -226,7 +293,7 @@
                 for p in range(group):
                     kept = jnp.where(ahead, q[p], before[p])
                     target[p, f, k] = kept - (value[p] - lower[p])
-        landed[pl.ds(f0, n), pl.ds(2 + base(first, me), height(first))] = target[me]
+        landed[block(c, owner, 2)] = target[me]
 
     ghosts = [
         remote(landed.at[:, pl.ds(2, 2)], landed.at[:, pl.ds(rows + 2, 2)], ghost_send, ghost_recv, (me, jnp.maximum(ring - 1, 0))),
@@ -238,27 +305,6 @@
         (below != above, bytes_of(landed.at[:, pl.ds(0, 2)], ghost_recv), bytes_of(landed.at[:, pl.ds(0, 2)], ghost_send)),
     ]
 
-    def radial(f):
-        def cell(i):
-            return landed[f, i]
-
-        q1, q2 = cell(1), cell(2)
-        d1 = q1 - cell(0)
-        d2 = q2 - q1
-        h1 = half_slope(d1, d2)
-        below = None
-        for j in range(rows + 1):
-            q3 = cell(j + 3)
-            d3 = q3 - q2
-            h2 = half_slope(d2, d3)
-            c, b = rate[j], bend[j]
-            ahead = c > 0.0
-            flux = c * jnp.where(ahead, q1, q2) + b * jnp.where(ahead, h1, h2)
-            if j > 0:
-                out[f, j - 1] = q1 - (flux - below)
-            below = flux
-            q1, q2, d2, h1 = q2, q3, d3, h2
-
     edges = 1 if more else count
 
     small[1].wait()
@@ -269,12 +315,25 @@
         pl.semaphore_wait(told, 1)
 
     tell(lifts, from_below, 1)
-    for c in range(count):
+    for c in range(full):
         arrive(c)
         with jax.named_scope("azimuth"):
-            azimuth(c)
+            azimuth(c, gathered[c], results[c], me)
         for d in peers():
-            back_copy(c, d).start()
+            if lending and c in (1,) and d is near[0]:
+                pl.when(jnp.logical_not(helps))(back_copy(c, d).start)
+            else:
+                back_copy(c, d).start()
+        if lending and c == 1:
+
+            @pl.when(helps)
+            def _():
+                with jax.named_scope("lent"):
+                    bytes_of(lent_in, lent_sem).wait_recv()
+                azimuth(full, lent_in, lent_out, 0)
+                for d in peers():
+                    give_back(d).start()
+
         if c == 0:
 
             @pl.when(lowers)
@@ -286,6 +345,20 @@
                 for d in peers():
                     pl.semaphore_signal(told, inc=1, device_id=(d, ring), device_id_type=MESH)
 
+    if lending:
+
+        @pl.when(keeps)
+        def _():
+            arrive(full)
+            azimuth(full, gathered[full], results[full], me)
+            for d in peers():
+                back_copy(full, d).start()
+
+        @pl.when(helps)
+        def _():
+            for c in (1,):
+                back_copy(c, near[0]).start()
+
     @pl.when(jnp.logical_not(leads))
     def _():
         pl.semaphore_wait(told, 1)
@@ -307,15 +380,20 @@
     for c in range(edges, count):
         first, f0, n = chunks[c]
         home(c)
-        with jax.named_scope("radial"):
-            for f in range(f0, f0 + n):
-                radial(f)
+        if f0 < out.shape[0]:
+            with jax.named_scope("radial"):
+                for f in range(f0, f0 + n):
+                    radial(landed, rate, bend, f, out, f)
     if not more:
-        for f in range(nf):
-            radial(f)
-
-    for phase in range(2):
-        bytes_of(own.at[:, pl.ds(0, rows - rows // group)], sent.at[phase]).wait_send()
+        for f in range(out.shape[0]):
+            radial(landed, rate, bend, f, out, f)
+
+    for c in range(full):
+        for phase in range(2):
+            bytes_of(results[c].at[pl.ds(0, group - 1)], sent.at[phase, c]).wait_send()
+    if lending:
+        for who, pieces in ((jnp.logical_not(keeps), 4), (helps, 8), (usual, 6)):
+            pl.when(who)(bytes_of(lent.at[pl.ds(0, pieces)], sent.at[0, full]).wait_send)
     for case, _, delivered in ghost_bytes:
         pl.when(case)(delivered.wait_send)
 
@@ -331,17 +409,23 @@
     ]
     count = len(chunks)
     dma = pltpu.SemaphoreType.DMA
+    lent = []
+    if lends(rows, group):
+        lent = [pltpu.VMEM((2 * group, 1, more, polar, width), jnp.float32), dma]
     operands = (fields, shift, fraction, radial_rate.T)
-    return pl.pallas_call(
+    left = chunks[-1][2]
+
+    def like(*shape):
+        return jax.ShapeDtypeStruct((*shape, polar, width), jnp.float32)
+
+    vmem, hbm = pl.BlockSpec(memory_space=pltpu.VMEM), pl.BlockSpec(memory_space=pltpu.HBM)
+    moved = pl.pallas_call(
         functools.partial(kernel, group, rings, chunks),
-        out_shape=jax.ShapeDtypeStruct(fields.shape, jnp.float32),
-        in_specs=[pl.BlockSpec(memory_space=pltpu.HBM)] * 4,
-        out_specs=pl.BlockSpec(memory_space=pltpu.VMEM),
+        out_shape=[like(nf - left, rows), like(nf, rows + 4), like(rows + 1), like(rows + 1)],
+        in_specs=[hbm] * 4,
+        out_specs=[vmem] * 4,
         scratch_shapes=[
             pltpu.VMEM((nf, rows, polar, width), jnp.float32),
-            pltpu.VMEM((nf, rows + 4, polar, width), jnp.float32),
-            pltpu.VMEM((rows + 1, polar, width), jnp.float32),
-            pltpu.VMEM((rows + 1, polar, width), jnp.float32),
             pltpu.SMEM(shift.shape, jnp.int32),
             pltpu.SMEM(fraction.shape, jnp.float32),
             pltpu.VMEM(radial_rate.shape[::-1], jnp.float32),
@@ -349,17 +433,26 @@
             *boxes,
             dma((3,)),
             dma((2,)),
-            dma((2,)),
+            dma((2, count)),
             dma((count,)),
             dma((count,)),
             dma,
             dma,
             *[pltpu.SemaphoreType.REGULAR] * 3,
+            *lent,
         ],
         compiler_params=pltpu.CompilerParams(
             collective_id=0, has_side_effects=True, vmem_limit_bytes=10 * fields.size * 4
         ),
     )(*(pltpu.with_memory_space_constraint(x, pltpu.HBM) for x in operands))
+    return pl.pallas_call(
+        finish,
+        out_shape=jax.ShapeDtypeStruct(fields.shape, jnp.float32),
+        in_specs=[vmem] * 4,
+        out_specs=hbm,
+        scratch_shapes=[pltpu.VMEM((left, rows, polar, width), jnp.float32), dma((2,))],
+        compiler_params=pltpu.CompilerParams(vmem_limit_bytes=5 * fields.size * 4),
+    )(*moved)
 
 
 def solution(mesh):

time: 27.6 us -> 27 us (0.978)
  local copies, waits for them, and re-layouts: 0.95 us -> 0 us
  Pallas kernels: 26.5 us -> 26.9 us
    pallas_call x0 -> x1, Pallas kernels: none -> 0.96 us  [shards(): pl.pallas_call(finish, out_shape=jax.ShapeDtypeStruct(fields.shape, jnp.f...]
    unnamed x1 -> x0, local copies, waits for them, and re-layouts: 0.95 us -> none
    pallas_call x1, Pallas kernels: 26.5 us -> 25.9 us  [shards(): pl.pallas_call(functools.partial(kernel, group, rings, chunks), out_shape...]
where the time goes in v3:
time: 27 us; the launch traced here: 26.9 us
  Pallas kernels  26.9 us (100%)
    pallas_call x1, Pallas kernels, shards(): pl.pallas_call(functools.partial(kernel, group, rings, chunks), out_shape...  25.9 us
    pallas_call x1, Pallas kernels, shards(): pl.pallas_call(finish, out_shape=jax.ShapeDtypeStruct(fields.shape, jnp.f...  0.96 us

profile of v3, /device:TPU:0, one launch (start us, length us, event | category | flops | bytes accessed | tf_op | source)
XLA Modules:
  0.0 26.9 jit_solution(18178498209035305021)
XLA Ops:
  0.0 25.9 %shard_map.46 = (f32[4,12,32,128]{3,2,1,0:T(8,128)S(1)}, f32[5,16,32,128]{3,2,1,0:T(8,128)S(1)}, f32[13,32,128]{2,1,0:T(8,128)S(1)}, f32[13,32,128]{2,1,0:T(8,128)S(1)}) custom-call(f32[5,12,32,128]{3,2,1,0:T(8,128)} %fields.1, s32[96]{0:T(128)} %shift_in.1, f32[96]{0:T(128)} %fraction_in.1, f32[32,96]{1,0:T(8,128)} %bitcast.1), custom_call_target="tpu_custom_call" | custom-call | tf_op jit(solution)/shard_map/pallas_call | solution.py:422
  25.9 1.0 %shard_map.47 = f32[5,12,32,128]{3,2,1,0:T(8,128)} custom-call(f32[4,12,32,128]{3,2,1,0:T(8,128)S(1)} %get-tuple-element.9.done, f32[5,16,32,128]{3,2,1,0:T(8,128)S(1)} %get-tuple-element.10.landed, f32[13,32,128]{2,1,0:T(8,128)S(1)} %get-tuple-element.11.rate, f32[13,32,128]{2,1,0:T(8,128)S(1)} %get-tuple-element.12.bend), custom_call_target="tpu_custom_call" | custom-call | tf_op jit(solution)/shard_map/pallas_call | solution.py:448

commit v4 on v3

--- a/solution.py
+++ b/solution.py
@@ -29,21 +29,20 @@
     return group == 4 and rows > group
 
 
-def radial(landed, rate, bend, f, target, g):
-    rows = rate.shape[0] - 1
-    q1, q2 = landed[f, 1], landed[f, 2]
-    d1 = q1 - landed[f, 0]
+def radial(landed, rate, bend, f, target, g, low, high):
+    q1, q2 = landed[f, low + 1], landed[f, low + 2]
+    d1 = q1 - landed[f, low]
     d2 = q2 - q1
     h1 = half_slope(d1, d2)
     inner = None
-    for j in range(rows + 1):
+    for j in range(low, high + 1):
         q3 = landed[f, j + 3]
         d3 = q3 - q2
         h2 = half_slope(d2, d3)
         c, b = rate[j], bend[j]
         ahead = c > 0.0
         flux = c * jnp.where(ahead, q1, q2) + b * jnp.where(ahead, h1, h2)
-        if j > 0:
+        if j > low:
             target[g, j - 1] = q1 - (flux - inner)
         inner = flux
         q1, q2, d2, h1 = q2, q3, d3, h2
@@ -55,7 +54,7 @@
     late = pltpu.make_async_copy(fresh, out.at[pl.ds(ready, fresh.shape[0])], sems.at[1])
     early.start()
     for g in range(fresh.shape[0]):
-        radial(landed, rate, bend, ready + g, fresh, g)
+        radial(landed, rate, bend, ready + g, fresh, g, 0, fresh.shape[1])
     late.start()
     early.wait()
     late.wait()
@@ -76,11 +75,13 @@
     own, shift, fraction, rates, *rest,
 ):
     count = len(chunks)
-    gathered, results = rest[:count], rest[count : 2 * count]
-    small_sem, in_sem, sent, gather_sem, home_sem, ghost_send, ghost_recv, passed, told, from_below, *lent = rest[2 * count :]
+    boxes, rest = rest[:count], rest[count:]
+    gathered = [box.at[pl.ds(0, group)] for box in boxes]
+    results = [box.at[pl.ds(group, group)] for box in boxes]
+    small_sem, in_sem, sent, gather_sem, home_sem, ghost_send, ghost_recv, passed, told, tied, *rest = rest
     lending = lends(fields.shape[1], group)
     if lending:
-        lent, lent_sem = lent
+        lent, lent_sem = rest
         lent_in, lent_out = lent.at[pl.ds(0, group)], lent.at[pl.ds(group, group)]
     nf, rows, polar, width = fields.shape
     me, ring = lax.axis_index("az"), lax.axis_index("rad")
@@ -100,21 +101,6 @@
         return pl.ds(f0, n), pl.ds(lift + base(first, d), height(first))
 
     near, far = peers_of(group, me)
-    barrier = pltpu.get_barrier_semaphore()
-    for d in near:
-        pl.semaphore_signal(barrier, inc=1, device_id=(d, ring), device_id_type=MESH)
-
-    below, above = ring > 0, ring < rings - 1
-    leads = me == 0
-
-    def tell(who, semaphore, step):
-        @pl.when(who)
-        def _():
-            pl.semaphore_signal(semaphore, inc=1, device_id=(me, ring + step), device_id_type=MESH)
-
-    lowers, lifts = jnp.logical_and(leads, below), jnp.logical_and(leads, above)
-    tell(lifts, barrier, 1)
-
     stages = [
         pltpu.make_async_copy(fields.at[:, pl.ds(0, group - 2)], own.at[:, pl.ds(0, group - 2)], in_sem.at[0]),
         pltpu.make_async_copy(fields.at[:, pl.ds(rows - 2, 2)], own.at[:, pl.ds(rows - 2, 2)], in_sem.at[0]),
@@ -129,6 +115,30 @@
         )
     for copy in stages:
         copy.start()
+
+    barrier = pltpu.get_barrier_semaphore()
+    between = jnp.logical_or(me == 1, me == 2)
+
+    def greet():
+        for d in near:
+            pl.semaphore_signal(barrier, inc=1, device_id=(d, ring), device_id_type=MESH)
+
+    if far:
+        pl.when(me != 3)(greet)
+    else:
+        greet()
+
+    below, above = ring > 0, ring < rings - 1
+    leads = me == 0
+
+    def tell(who, semaphore, step):
+        @pl.when(who)
+        def _():
+            pl.semaphore_signal(semaphore, inc=1, device_id=(me, ring + step), device_id_type=MESH)
+
+    lowers, lifts = jnp.logical_and(leads, below), jnp.logical_and(leads, above)
+    tell(lifts, barrier, 1)
+
     lender = ring == 0
     keeps = jnp.logical_or(me != 0, jnp.logical_not(lender))
     helps = jnp.logical_and(me == 3, lender)
@@ -156,9 +166,14 @@
         copy.start()
 
     with jax.named_scope("barrier"):
-        pl.semaphore_wait(barrier, len(near) + jnp.where(lowers, 1, 0))
+        greeted = jnp.where(between, 1, 2) if far else len(near)
+        pl.semaphore_wait(barrier, greeted + jnp.where(lowers, 1, 0))
     if far:
-        pl.semaphore_signal(passed, inc=1, device_id=(near[0], ring), device_id_type=MESH)
+
+        @pl.when(me == 3)
+        def _():
+            for d in near:
+                pl.semaphore_signal(tied, inc=1, device_id=(d, ring), device_id_type=MESH)
 
     def remote(src, dst, send_sem, recv_sem, device):
         return pltpu.make_async_remote_copy(
@@ -167,20 +182,21 @@
         )
 
     def out_copy(c, d):
-        return remote(
-            own.at[block(c, d)], gathered[c].at[me], sent.at[0, c], gather_sem.at[c], (d, ring)
-        )
+        return remote(own.at[block(c, d)], gathered[c].at[me], sent.at[c], gather_sem.at[c], (d, ring))
+
+    edge_sems = [home_sem.at[i] for i in (0, count, count + 1)] if lending else []
 
     def back_copy(c, d):
-        return remote(
-            results[c].at[d], landed.at[block(c, me, 2)], sent.at[1 if c < full else 0, c], home_sem.at[c], (d, ring)
-        )
+        landing = home_sem.at[c]
+        if lending and c == 0:
+            landing = edge_sems[[d is other for other in near + far].index(True)]
+        return remote(results[c].at[d], landed.at[block(c, me, 2)], sent.at[c], landing, (d, ring))
 
     def lend():
-        return remote(own.at[block(full, 0)], lent_in.at[me], sent.at[0, full], lent_sem, (3, ring))
+        return remote(own.at[block(full, 0)], lent_in.at[me], sent.at[full], lent_sem, (3, ring))
 
     def give_back(d):
-        return remote(lent_out.at[d], landed.at[block(full, 0, 2)], sent.at[0, full], home_sem.at[full], (d, ring))
+        return remote(lent_out.at[d], landed.at[block(full, 0, 2)], sent.at[full], home_sem.at[full], (d, ring))
 
     def bytes_of(ref, semaphore):
         return remote(ref, ref, semaphore, semaphore, (me, ring))
@@ -207,13 +223,30 @@
             stages[2].wait()
 
     started = min(2, count)
-    for c in range(started):
-        ready(c)
-        for d in near:
-            out_copy(c, d).start()
     if far:
+        known = [jnp.logical_or(jnp.logical_not(between), me == k + 1) for k in range(2)]
+        for c in range(started):
+            with jax.named_scope("ready"):
+                ready(c)
+            for k in range(2):
+                pl.when(known[k])(out_copy(c, near[k]).start)
+
+        @pl.when(between)
+        def _():
+            with jax.named_scope("answer"):
+                pl.semaphore_wait(tied, 1)
+            for c in range(started):
+                for k in range(2):
+                    pl.when(me != k + 1)(out_copy(c, near[k]).start)
+
+        pl.semaphore_signal(passed, inc=1, device_id=(near[0], ring), device_id_type=MESH)
         with jax.named_scope("passed"):
             pl.semaphore_wait(passed, 1)
+    else:
+        for c in range(started):
+            ready(c)
+            for d in near:
+                out_copy(c, d).start()
     tell(lowers, told, -1)
     for c in range(started):
         for d in far:
@@ -295,10 +328,6 @@
                     target[p, f, k] = kept - (value[p] - lower[p])
         landed[block(c, owner, 2)] = target[me]
 
-    ghosts = [
-        remote(landed.at[:, pl.ds(2, 2)], landed.at[:, pl.ds(rows + 2, 2)], ghost_send, ghost_recv, (me, jnp.maximum(ring - 1, 0))),
-        remote(landed.at[:, pl.ds(rows, 2)], landed.at[:, pl.ds(0, 2)], ghost_send, ghost_recv, (me, jnp.minimum(ring + 1, rings - 1))),
-    ]
     inside = jnp.logical_and(below, above)
     ghost_bytes = [
         (inside, bytes_of(landed.at[:, pl.ds(0, 4)], ghost_recv), bytes_of(landed.at[:, pl.ds(0, 4)], ghost_send)),
@@ -314,14 +343,19 @@
     def _():
         pl.semaphore_wait(told, 1)
 
-    tell(lifts, from_below, 1)
+    tell(lifts, tied, 1)
     for c in range(full):
         arrive(c)
         with jax.named_scope("azimuth"):
             azimuth(c, gathered[c], results[c], me)
+        if lending and c == 2:
+            for d in (far[0], near[1]):
+                pl.when(me == 0)(back_copy(1, d).start)
         for d in peers():
-            if lending and c in (1,) and d is near[0]:
+            if lending and c in (1, 2) and d is near[0]:
                 pl.when(jnp.logical_not(helps))(back_copy(c, d).start)
+            elif lending and c == 1 and d is not near[0]:
+                pl.when(me != 0)(back_copy(c, d).start)
             else:
                 back_copy(c, d).start()
         if lending and c == 1:
@@ -331,14 +365,14 @@
                 with jax.named_scope("lent"):
                     bytes_of(lent_in, lent_sem).wait_recv()
                 azimuth(full, lent_in, lent_out, 0)
-                for d in peers():
+                for d in (far[0], near[1]):
                     give_back(d).start()
 
         if c == 0:
 
             @pl.when(lowers)
             def _():
-                pl.semaphore_wait(from_below, 1)
+                pl.semaphore_wait(tied, 1)
 
             @pl.when(leads)
             def _():
@@ -352,48 +386,80 @@
             arrive(full)
             azimuth(full, gathered[full], results[full], me)
             for d in peers():
-                back_copy(full, d).start()
+                if d is near[0]:
+                    pl.when(jnp.logical_not(helps))(back_copy(full, d).start)
+                else:
+                    back_copy(full, d).start()
 
         @pl.when(helps)
         def _():
-            for c in (1,):
+            for c in (1, 2):
                 back_copy(c, near[0]).start()
+            back_copy(full, near[0]).start()
+            give_back(near[0]).start()
 
     @pl.when(jnp.logical_not(leads))
     def _():
         pl.semaphore_wait(told, 1)
 
-    for c in range(edges):
-        home(c)
-
-    @pl.when(below)
-    def _():
-        ghosts[0].start()
-
-    @pl.when(above)
-    def _():
-        ghosts[1].start()
-
-    for case, received, _ in ghost_bytes:
-        pl.when(case)(received.wait_recv)
-
-    for c in range(edges, count):
-        first, f0, n = chunks[c]
-        home(c)
-        if f0 < out.shape[0]:
-            with jax.named_scope("radial"):
-                for f in range(f0, f0 + n):
-                    radial(landed, rate, bend, f, out, f)
-    if not more:
-        for f in range(out.shape[0]):
-            radial(landed, rate, bend, f, out, f)
+    def edge_ghost(d):
+        down = d < 2
+        row = 2 + base(True, d)
+        target = jnp.where(down, rows + 2 + d, d - 2)
+        beside = jnp.clip(ring + jnp.where(down, -1, 1), 0, rings - 1)
+        copy = remote(
+            landed.at[:, pl.ds(row, 1)], landed.at[:, pl.ds(target, 1)], ghost_send, ghost_recv, (me, beside)
+        )
+        pl.when(jnp.where(down, ring, rings - 1 - ring) > 0)(copy.start)
+
+    if lending:
+        edge_ghost(me)
+        for k, d in enumerate(near + far):
+            with jax.named_scope("edge%d" % k):
+                bytes_of(results[0].at[0], edge_sems[k]).wait_recv()
+            edge_ghost(d)
+    else:
+        for c in range(edges):
+            home(c)
+        for there, row, target, step in ((below, 2, rows + 2, -1), (above, rows, 0, 1)):
+            beside = jnp.clip(ring + step, 0, rings - 1)
+            copy = remote(
+                landed.at[:, pl.ds(row, 2)], landed.at[:, pl.ds(target, 2)], ghost_send, ghost_recv, (me, beside)
+            )
+            pl.when(there)(copy.start)
+
+    def advance(low_field, fields_in, spans):
+        for f in range(low_field, low_field + fields_in):
+            for low, high in spans:
+                radial(landed, rate, bend, f, out, f, low, high)
+
+    def ghosts_in():
+        for case, received, _ in ghost_bytes:
+            pl.when(case)(received.wait_recv)
+
+    done = out.shape[0]
+    if more and rows > 5:
+        _, f0, n = chunks[1]
+        home(1)
+        advance(f0, n, [(2, rows - 2)])
+        ghosts_in()
+        advance(f0, n, [(0, 2), (rows - 2, rows)])
+        for c in range(2, count):
+            _, f0, n = chunks[c]
+            home(c)
+            if f0 < done:
+                advance(f0, n, [(0, rows)])
+    else:
+        for c in range(edges, count):
+            home(c)
+        ghosts_in()
+        advance(0, done, [(0, rows)])
 
     for c in range(full):
-        for phase in range(2):
-            bytes_of(results[c].at[pl.ds(0, group - 1)], sent.at[phase, c]).wait_send()
+        bytes_of(boxes[c].at[pl.ds(0, 2 * (group - 1))], sent.at[c]).wait_send()
     if lending:
         for who, pieces in ((jnp.logical_not(keeps), 4), (helps, 8), (usual, 6)):
-            pl.when(who)(bytes_of(lent.at[pl.ds(0, pieces)], sent.at[0, full]).wait_send)
+            pl.when(who)(bytes_of(lent.at[pl.ds(0, pieces)], sent.at[full]).wait_send)
     for case, _, delivered in ghost_bytes:
         pl.when(case)(delivered.wait_send)
 
@@ -404,7 +470,7 @@
     chunks = chunks_of(nf, rows, group)
     more = rows // group - 1
     boxes = [
-        pltpu.VMEM((group, n, 1 if first else more, polar, width), jnp.float32)
+        pltpu.VMEM((2 * group, n, 1 if first else more, polar, width), jnp.float32)
         for first, f0, n in chunks
     ]
     count = len(chunks)
@@ -430,12 +496,11 @@
             pltpu.SMEM(fraction.shape, jnp.float32),
             pltpu.VMEM(radial_rate.shape[::-1], jnp.float32),
             *boxes,
-            *boxes,
             dma((3,)),
             dma((2,)),
-            dma((2, count)),
             dma((count,)),
             dma((count,)),
+            dma((count + 2 * lends(rows, group),)),
             dma,
             dma,
             *[pltpu.SemaphoreType.REGULAR] * 3,

time: 27 us -> 26.8 us (level)
  Pallas kernels: 26.9 us -> 26.6 us
where the time goes in v4:
time: 26.8 us; the launch traced here: 26.6 us
  Pallas kernels  26.6 us (99%)
    pallas_call x1, Pallas kernels, shards(): pl.pallas_call(functools.partial(kernel, group, rings, chunks), out_shape...  25.6 us
    pallas_call x1, Pallas kernels, shards(): pl.pallas_call(finish, out_shape=jax.ShapeDtypeStruct(fields.shape, jnp.f...  0.96 us

profile of v4, /device:TPU:0, one launch (start us, length us, event | category | flops | bytes accessed | tf_op | source)
XLA Modules:
  0.0 26.6 jit_solution(15399320587542070328)
XLA Ops:
  0.0 25.6 %shard_map.46 = (f32[4,12,32,128]{3,2,1,0:T(8,128)S(1)}, f32[5,16,32,128]{3,2,1,0:T(8,128)S(1)}, f32[13,32,128]{2,1,0:T(8,128)S(1)}, f32[13,32,128]{2,1,0:T(8,128)S(1)}) custom-call(f32[5,12,32,128]{3,2,1,0:T(8,128)} %fields.1, s32[96]{0:T(128)} %shift_in.1, f32[96]{0:T(128)} %fraction_in.1, f32[32,96]{1,0:T(8,128)} %bitcast.1), custom_call_target="tpu_custom_call" | custom-call | tf_op jit(solution)/shard_map/pallas_call | solution.py:488
  25.7 1.0 %shard_map.47 = f32[5,12,32,128]{3,2,1,0:T(8,128)} custom-call(f32[4,12,32,128]{3,2,1,0:T(8,128)S(1)} %get-tuple-element.9.done, f32[5,16,32,128]{3,2,1,0:T(8,128)S(1)} %get-tuple-element.10.landed, f32[13,32,128]{2,1,0:T(8,128)S(1)} %get-tuple-element.11.rate, f32[13,32,128]{2,1,0:T(8,128)S(1)} %get-tuple-element.12.bend), custom_call_target="tpu_custom_call" | custom-call | tf_op jit(solution)/shard_map/pallas_call | solution.py:513

commit v5 on v4

--- a/solution.py
+++ b/solution.py
@@ -72,13 +72,13 @@
     group, rings, chunks,
     fields, shift_in, fraction_in, rates_in,
     out, landed, rate, bend,
-    own, shift, fraction, rates, *rest,
+    shift, fraction, rates, *rest,
 ):
     count = len(chunks)
     boxes, rest = rest[:count], rest[count:]
     gathered = [box.at[pl.ds(0, group)] for box in boxes]
     results = [box.at[pl.ds(group, group)] for box in boxes]
-    small_sem, in_sem, sent, gather_sem, home_sem, ghost_send, ghost_recv, passed, told, tied, *rest = rest
+    small_sem, sent, gather_sem, home_sem, ghost_send, ghost_recv, passed, told, tied, *rest = rest
     lending = lends(fields.shape[1], group)
     if lending:
         lent, lent_sem = rest
@@ -101,21 +101,6 @@
         return pl.ds(f0, n), pl.ds(lift + base(first, d), height(first))
 
     near, far = peers_of(group, me)
-    stages = [
-        pltpu.make_async_copy(fields.at[:, pl.ds(0, group - 2)], own.at[:, pl.ds(0, group - 2)], in_sem.at[0]),
-        pltpu.make_async_copy(fields.at[:, pl.ds(rows - 2, 2)], own.at[:, pl.ds(rows - 2, 2)], in_sem.at[0]),
-    ]
-    if more:
-        stages.append(
-            pltpu.make_async_copy(
-                fields.at[:, pl.ds(group - 2, rows - group)],
-                own.at[:, pl.ds(group - 2, rows - group)],
-                in_sem.at[1],
-            )
-        )
-    for copy in stages:
-        copy.start()
-
     barrier = pltpu.get_barrier_semaphore()
     between = jnp.logical_or(me == 1, me == 2)
 
@@ -182,7 +167,7 @@
         )
 
     def out_copy(c, d):
-        return remote(own.at[block(c, d)], gathered[c].at[me], sent.at[c], gather_sem.at[c], (d, ring))
+        return remote(fields.at[block(c, d)], gathered[c].at[me], sent.at[c], gather_sem.at[c], (d, ring))
 
     edge_sems = [home_sem.at[i] for i in (0, count, count + 1)] if lending else []
 
@@ -193,7 +178,7 @@
         return remote(results[c].at[d], landed.at[block(c, me, 2)], sent.at[c], landing, (d, ring))
 
     def lend():
-        return remote(own.at[block(full, 0)], lent_in.at[me], sent.at[full], lent_sem, (3, ring))
+        return remote(fields.at[block(full, 0)], lent_in.at[me], sent.at[full], lent_sem, (3, ring))
 
     def give_back(d):
         return remote(lent_out.at[d], landed.at[block(full, 0, 2)], sent.at[full], home_sem.at[full], (d, ring))
@@ -216,18 +201,10 @@
     def peers():
         return far + near
 
-    def ready(c):
-        if c == 0:
-            bytes_of(own.at[:, pl.ds(0, group)], in_sem.at[0]).wait_recv()
-        if c == 1 and more:
-            stages[2].wait()
-
     started = min(2, count)
     if far:
         known = [jnp.logical_or(jnp.logical_not(between), me == k + 1) for k in range(2)]
         for c in range(started):
-            with jax.named_scope("ready"):
-                ready(c)
             for k in range(2):
                 pl.when(known[k])(out_copy(c, near[k]).start)
 
@@ -244,7 +221,6 @@
             pl.semaphore_wait(passed, 1)
     else:
         for c in range(started):
-            ready(c)
             for d in near:
                 out_copy(c, d).start()
     tell(lowers, told, -1)
@@ -491,13 +467,11 @@
         in_specs=[hbm] * 4,
         out_specs=[vmem] * 4,
         scratch_shapes=[
-            pltpu.VMEM((nf, rows, polar, width), jnp.float32),
             pltpu.SMEM(shift.shape, jnp.int32),
             pltpu.SMEM(fraction.shape, jnp.float32),
             pltpu.VMEM(radial_rate.shape[::-1], jnp.float32),
             *boxes,
             dma((3,)),
-            dma((2,)),
             dma((count,)),
             dma((count,)),
             dma((count + 2 * lends(rows, group),)),

time: 26.8 us -> 26.3 us (0.981)
  Pallas kernels: 26.6 us -> 25.9 us
    pallas_call x1, Pallas kernels: 25.6 us -> 24.9 us  [shards(): pl.pallas_call(functools.partial(kernel, group, rings, chunks), out_shape...]
where the time goes in v5:
time: 26.3 us; the launch traced here: 25.9 us
  Pallas kernels  25.9 us (98%)
    pallas_call x1, Pallas kernels, shards(): pl.pallas_call(functools.partial(kernel, group, rings, chunks), out_shape...  24.9 us
    pallas_call x1, Pallas kernels, shards(): pl.pallas_call(finish, out_shape=jax.ShapeDtypeStruct(fields.shape, jnp.f...  0.96 us

profile of v5, /device:TPU:0, one launch (start us, length us, event | category | flops | bytes accessed | tf_op | source)
XLA Modules:
  0.0 25.9 jit_solution(4552349371080704517)
XLA Ops:
  0.0 24.9 %shard_map.46 = (f32[4,12,32,128]{3,2,1,0:T(8,128)S(1)}, f32[5,16,32,128]{3,2,1,0:T(8,128)S(1)}, f32[13,32,128]{2,1,0:T(8,128)S(1)}, f32[13,32,128]{2,1,0:T(8,128)S(1)}) custom-call(f32[5,12,32,128]{3,2,1,0:T(8,128)} %fields.1, s32[96]{0:T(128)} %shift_in.1, f32[96]{0:T(128)} %fraction_in.1, f32[32,96]{1,0:T(8,128)} %bitcast.1), custom_call_target="tpu_custom_call" | custom-call | tf_op jit(solution)/shard_map/pallas_call | solution.py:464
  25.0 1.0 %shard_map.47 = f32[5,12,32,128]{3,2,1,0:T(8,128)} custom-call(f32[4,12,32,128]{3,2,1,0:T(8,128)S(1)} %get-tuple-element.9.done, f32[5,16,32,128]{3,2,1,0:T(8,128)S(1)} %get-tuple-element.10.landed, f32[13,32,128]{2,1,0:T(8,128)S(1)} %get-tuple-element.11.rate, f32[13,32,128]{2,1,0:T(8,128)S(1)} %get-tuple-element.12.bend), custom_call_target="tpu_custom_call" | custom-call | tf_op jit(solution)/shard_map/pallas_call | solution.py:487

commit v6 on v5

--- a/solution.py
+++ b/solution.py
@@ -201,39 +201,32 @@
     def peers():
         return far + near
 
-    started = min(2, count)
     if far:
         known = [jnp.logical_or(jnp.logical_not(between), me == k + 1) for k in range(2)]
-        for c in range(started):
-            for k in range(2):
-                pl.when(known[k])(out_copy(c, near[k]).start)
+        for k in range(2):
+            pl.when(known[k])(out_copy(0, near[k]).start)
 
         @pl.when(between)
         def _():
             with jax.named_scope("answer"):
                 pl.semaphore_wait(tied, 1)
-            for c in range(started):
-                for k in range(2):
-                    pl.when(me != k + 1)(out_copy(c, near[k]).start)
+            for k in range(2):
+                pl.when(me != k + 1)(out_copy(0, near[k]).start)
 
         pl.semaphore_signal(passed, inc=1, device_id=(near[0], ring), device_id_type=MESH)
         with jax.named_scope("passed"):
             pl.semaphore_wait(passed, 1)
     else:
-        for c in range(started):
-            for d in near:
-                out_copy(c, d).start()
+        for d in near:
+            out_copy(0, d).start()
     tell(lowers, told, -1)
-    for c in range(started):
-        for d in far:
+    for c in range(full):
+        for d in far + near if c else far:
             out_copy(c, d).start()
-    if lending:
-        pl.when(jnp.logical_and(lender, me != 3))(lend().start)
-    for c in range(started, full):
-        for d in near + far:
-            out_copy(c, d).start()
-    if lending:
-        for d in near + far:
+        if lending and c == 1:
+            pl.when(jnp.logical_and(lender, me != 3))(lend().start)
+    if lending:
+        for d in far + near:
             pl.when(jnp.logical_or(d != 0, jnp.logical_not(lender)))(out_copy(full, d).start)
 
     small[0].wait()
@@ -325,13 +318,13 @@
         with jax.named_scope("azimuth"):
             azimuth(c, gathered[c], results[c], me)
         if lending and c == 2:
-            for d in (far[0], near[1]):
-                pl.when(me == 0)(back_copy(1, d).start)
+            pl.when(me < 2)(back_copy(1, far[0]).start)
+            pl.when(me == 0)(back_copy(1, near[1]).start)
         for d in peers():
             if lending and c in (1, 2) and d is near[0]:
                 pl.when(jnp.logical_not(helps))(back_copy(c, d).start)
             elif lending and c == 1 and d is not near[0]:
-                pl.when(me != 0)(back_copy(c, d).start)
+                pl.when(me > 1 if d is far[0] else me != 0)(back_copy(c, d).start)
             else:
                 back_copy(c, d).start()
         if lending and c == 1:

time: 26.3 us -> 26.3 us (level)
  no operation moved by 1% of the time
where the time goes in v6:
time: 26.3 us; the launch traced here: 25.9 us
  Pallas kernels  25.9 us (98%)
    pallas_call x1, Pallas kernels, shards(): pl.pallas_call(functools.partial(kernel, group, rings, chunks), out_shape...  25 us
    pallas_call x1, Pallas kernels, shards(): pl.pallas_call(finish, out_shape=jax.ShapeDtypeStruct(fields.shape, jnp.f...  0.96 us

profile of v6, /device:TPU:0, one launch (start us, length us, event | category | flops | bytes accessed | tf_op | source)
XLA Modules:
  0.0 25.9 jit_solution(3050949043403979377)
XLA Ops:
  0.0 25.0 %shard_map.46 = (f32[4,12,32,128]{3,2,1,0:T(8,128)S(1)}, f32[5,16,32,128]{3,2,1,0:T(8,128)S(1)}, f32[13,32,128]{2,1,0:T(8,128)S(1)}, f32[13,32,128]{2,1,0:T(8,128)S(1)}) custom-call(f32[5,12,32,128]{3,2,1,0:T(8,128)} %fields.1, s32[96]{0:T(128)} %shift_in.1, f32[96]{0:T(128)} %fraction_in.1, f32[32,96]{1,0:T(8,128)} %bitcast.1), custom_call_target="tpu_custom_call" | custom-call | tf_op jit(solution)/shard_map/pallas_call | solution.py:457
  25.0 1.0 %shard_map.47 = f32[5,12,32,128]{3,2,1,0:T(8,128)} custom-call(f32[4,12,32,128]{3,2,1,0:T(8,128)S(1)} %get-tuple-element.9.done, f32[5,16,32,128]{3,2,1,0:T(8,128)S(1)} %get-tuple-element.10.landed, f32[13,32,128]{2,1,0:T(8,128)S(1)} %get-tuple-element.11.rate, f32[13,32,128]{2,1,0:T(8,128)S(1)} %get-tuple-element.12.bend), custom_call_target="tpu_custom_call" | custom-call | tf_op jit(solution)/shard_map/pallas_call | solution.py:480

commit v7 on v6

--- a/solution.py
+++ b/solution.py
@@ -128,6 +128,7 @@
     keeps = jnp.logical_or(me != 0, jnp.logical_not(lender))
     helps = jnp.logical_and(me == 3, lender)
     usual = jnp.logical_and(keeps, jnp.logical_not(helps))
+    defers = jnp.logical_and(me > 1, lax.rem(ring, 2) == 0)
 
     def own_copy(c):
         return pltpu.make_async_copy(fields.at[block(c, me)], gathered[c].at[me], gather_sem.at[c])
@@ -322,7 +323,7 @@
             pl.when(me == 0)(back_copy(1, near[1]).start)
         for d in peers():
             if lending and c in (1, 2) and d is near[0]:
-                pl.when(jnp.logical_not(helps))(back_copy(c, d).start)
+                pl.when(jnp.logical_not(defers))(back_copy(c, d).start)
             elif lending and c == 1 and d is not near[0]:
                 pl.when(me > 1 if d is far[0] else me != 0)(back_copy(c, d).start)
             else:
@@ -356,16 +357,16 @@
             azimuth(full, gathered[full], results[full], me)
             for d in peers():
                 if d is near[0]:
-                    pl.when(jnp.logical_not(helps))(back_copy(full, d).start)
+                    pl.when(jnp.logical_not(defers))(back_copy(full, d).start)
                 else:
                     back_copy(full, d).start()
 
-        @pl.when(helps)
-        def _():
-            for c in (1, 2):
+        @pl.when(defers)
+        def _():
+            for c in (*(1, 2), full):
                 back_copy(c, near[0]).start()
-            back_copy(full, near[0]).start()
-            give_back(near[0]).start()
+
+        pl.when(helps)(give_back(near[0]).start)
 
     @pl.when(jnp.logical_not(leads))
     def _():

time: 26.3 us -> 26.1 us (level)
  no operation moved by 1% of the time
where the time goes in v7:
time: 26.1 us; the launch traced here: 25.9 us
  Pallas kernels  25.9 us (99%)
    pallas_call x1, Pallas kernels, shards(): pl.pallas_call(functools.partial(kernel, group, rings, chunks), out_shape...  25 us
    pallas_call x1, Pallas kernels, shards(): pl.pallas_call(finish, out_shape=jax.ShapeDtypeStruct(fields.shape, jnp.f...  0.96 us

profile of v7, /device:TPU:0, one launch (start us, length us, event | category | flops | bytes accessed | tf_op | source)
XLA Modules:
  0.0 25.9 jit_solution(4476025750996323255)
XLA Ops:
  0.0 25.0 %shard_map.46 = (f32[4,12,32,128]{3,2,1,0:T(8,128)S(1)}, f32[5,16,32,128]{3,2,1,0:T(8,128)S(1)}, f32[13,32,128]{2,1,0:T(8,128)S(1)}, f32[13,32,128]{2,1,0:T(8,128)S(1)}) custom-call(f32[5,12,32,128]{3,2,1,0:T(8,128)} %fields.1, s32[96]{0:T(128)} %shift_in.1, f32[96]{0:T(128)} %fraction_in.1, f32[32,96]{1,0:T(8,128)} %bitcast.1), custom_call_target="tpu_custom_call" | custom-call | tf_op jit(solution)/shard_map/pallas_call | solution.py:458
  25.0 1.0 %shard_map.47 = f32[5,12,32,128]{3,2,1,0:T(8,128)} custom-call(f32[4,12,32,128]{3,2,1,0:T(8,128)S(1)} %get-tuple-element.9.done, f32[5,16,32,128]{3,2,1,0:T(8,128)S(1)} %get-tuple-element.10.landed, f32[13,32,128]{2,1,0:T(8,128)S(1)} %get-tuple-element.11.rate, f32[13,32,128]{2,1,0:T(8,128)S(1)} %get-tuple-element.12.bend), custom_call_target="tpu_custom_call" | custom-call | tf_op jit(solution)/shard_map/pallas_call | solution.py:481

commit v8 on v7

--- a/solution.py
+++ b/solution.py
@@ -328,7 +328,7 @@
                 pl.when(me > 1 if d is far[0] else me != 0)(back_copy(c, d).start)
             else:
                 back_copy(c, d).start()
-        if lending and c == 1:
+        if lending and c == 2:
 
             @pl.when(helps)
             def _():

time: 26.1 us -> 26.1 us (level)
  no operation moved by 1% of the time
where the time goes in v8:
time: 26.1 us; the launch traced here: 25.9 us
  Pallas kernels  25.9 us (99%)
    pallas_call x1, Pallas kernels, shards(): pl.pallas_call(functools.partial(kernel, group, rings, chunks), out_shape...  25 us
    pallas_call x1, Pallas kernels, shards(): pl.pallas_call(finish, out_shape=jax.ShapeDtypeStruct(fields.shape, jnp.f...  0.96 us

profile of v8, /device:TPU:0, one launch (start us, length us, event | category | flops | bytes accessed | tf_op | source)
XLA Modules:
  0.0 25.9 jit_solution(9754706258004016396)
XLA Ops:
  0.0 25.0 %shard_map.46 = (f32[4,12,32,128]{3,2,1,0:T(8,128)S(1)}, f32[5,16,32,128]{3,2,1,0:T(8,128)S(1)}, f32[13,32,128]{2,1,0:T(8,128)S(1)}, f32[13,32,128]{2,1,0:T(8,128)S(1)}) custom-call(f32[5,12,32,128]{3,2,1,0:T(8,128)} %fields.1, s32[96]{0:T(128)} %shift_in.1, f32[96]{0:T(128)} %fraction_in.1, f32[32,96]{1,0:T(8,128)} %bitcast.1), custom_call_target="tpu_custom_call" | custom-call | tf_op jit(solution)/shard_map/pallas_call | solution.py:458
  25.0 1.0 %shard_map.47 = f32[5,12,32,128]{3,2,1,0:T(8,128)} custom-call(f32[4,12,32,128]{3,2,1,0:T(8,128)S(1)} %get-tuple-element.9.done, f32[5,16,32,128]{3,2,1,0:T(8,128)S(1)} %get-tuple-element.10.landed, f32[13,32,128]{2,1,0:T(8,128)S(1)} %get-tuple-element.11.rate, f32[13,32,128]{2,1,0:T(8,128)S(1)} %get-tuple-element.12.bend), custom_call_target="tpu_custom_call" | custom-call | tf_op jit(solution)/shard_map/pallas_call | solution.py:481

commit v9 on v8

--- a/solution.py
+++ b/solution.py
@@ -72,7 +72,7 @@
     group, rings, chunks,
     fields, shift_in, fraction_in, rates_in,
     out, landed, rate, bend,
-    shift, fraction, rates, *rest,
+    shift, fraction, rates, tally, *rest,
 ):
     count = len(chunks)
     boxes, rest = rest[:count], rest[count:]
@@ -168,7 +168,7 @@
         )
 
     def out_copy(c, d):
-        return remote(fields.at[block(c, d)], gathered[c].at[me], sent.at[c], gather_sem.at[c], (d, ring))
+        return remote(fields.at[block(c, d)], gathered[c].at[me], sent, gather_sem.at[c], (d, ring))
 
     edge_sems = [home_sem.at[i] for i in (0, count, count + 1)] if lending else []
 
@@ -176,13 +176,13 @@
         landing = home_sem.at[c]
         if lending and c == 0:
             landing = edge_sems[[d is other for other in near + far].index(True)]
-        return remote(results[c].at[d], landed.at[block(c, me, 2)], sent.at[c], landing, (d, ring))
+        return remote(results[c].at[d], landed.at[block(c, me, 2)], sent, landing, (d, ring))
 
     def lend():
-        return remote(fields.at[block(full, 0)], lent_in.at[me], sent.at[full], lent_sem, (3, ring))
+        return remote(fields.at[block(full, 0)], lent_in.at[me], sent, lent_sem, (3, ring))
 
     def give_back(d):
-        return remote(lent_out.at[d], landed.at[block(full, 0, 2)], sent.at[full], home_sem.at[full], (d, ring))
+        return remote(lent_out.at[d], landed.at[block(full, 0, 2)], sent, home_sem.at[full], (d, ring))
 
     def bytes_of(ref, semaphore):
         return remote(ref, ref, semaphore, semaphore, (me, ring))
@@ -425,11 +425,13 @@
         ghosts_in()
         advance(0, done, [(0, rows)])
 
-    for c in range(full):
-        bytes_of(boxes[c].at[pl.ds(0, 2 * (group - 1))], sent.at[c]).wait_send()
-    if lending:
+    always = 2 * (group - 1) * sum(n * height(first) for first, _, n in chunks[:full])
+    if lending:
+        piece = chunks[full][2] * more
         for who, pieces in ((jnp.logical_not(keeps), 4), (helps, 8), (usual, 6)):
-            pl.when(who)(bytes_of(lent.at[pl.ds(0, pieces)], sent.at[full]).wait_send)
+            pl.when(who)(bytes_of(tally.at[pl.ds(0, always + pieces * piece)], sent).wait_send)
+    else:
+        bytes_of(tally.at[pl.ds(0, always)], sent).wait_send()
     for case, _, delivered in ghost_bytes:
         pl.when(case)(delivered.wait_send)
 
@@ -464,9 +466,10 @@
             pltpu.SMEM(shift.shape, jnp.int32),
             pltpu.SMEM(fraction.shape, jnp.float32),
             pltpu.VMEM(radial_rate.shape[::-1], jnp.float32),
+            pltpu.VMEM((2 * group * nf * (1 + more), polar, width), jnp.float32),
             *boxes,
             dma((3,)),
-            dma((count,)),
+            dma,
             dma((count,)),
             dma((count + 2 * lends(rows, group),)),
             dma,

time: 26.1 us -> 26 us (level)
  no operation moved by 1% of the time
where the time goes in v9:
time: 26 us; the launch traced here: 25.9 us
  Pallas kernels  25.9 us (100%)
    pallas_call x1, Pallas kernels, shards(): pl.pallas_call(functools.partial(kernel, group, rings, chunks), out_shape...  24.9 us
    pallas_call x1, Pallas kernels, shards(): pl.pallas_call(finish, out_shape=jax.ShapeDtypeStruct(fields.shape, jnp.f...  0.96 us

profile of v9, /device:TPU:0, one launch (start us, length us, event | category | flops | bytes accessed | tf_op | source)
XLA Modules:
  0.0 25.9 jit_solution(12343084779721047980)
XLA Ops:
  0.0 24.9 %shard_map.46 = (f32[4,12,32,128]{3,2,1,0:T(8,128)S(1)}, f32[5,16,32,128]{3,2,1,0:T(8,128)S(1)}, f32[13,32,128]{2,1,0:T(8,128)S(1)}, f32[13,32,128]{2,1,0:T(8,128)S(1)}) custom-call(f32[5,12,32,128]{3,2,1,0:T(8,128)} %fields.1, s32[96]{0:T(128)} %shift_in.1, f32[96]{0:T(128)} %fraction_in.1, f32[32,96]{1,0:T(8,128)} %bitcast.1), custom_call_target="tpu_custom_call" | custom-call | tf_op jit(solution)/shard_map/pallas_call | solution.py:460
  24.9 1.0 %shard_map.47 = f32[5,12,32,128]{3,2,1,0:T(8,128)} custom-call(f32[4,12,32,128]{3,2,1,0:T(8,128)S(1)} %get-tuple-element.9.done, f32[5,16,32,128]{3,2,1,0:T(8,128)S(1)} %get-tuple-element.10.landed, f32[13,32,128]{2,1,0:T(8,128)S(1)} %get-tuple-element.11.rate, f32[13,32,128]{2,1,0:T(8,128)S(1)} %get-tuple-element.12.bend), custom_call_target="tpu_custom_call" | custom-call | tf_op jit(solution)/shard_map/pallas_call | solution.py:484
